TPU v7x, 512 devices: a whole 4x8x8 slice. The times are simulated.
512 devices in a mesh: grp: 8 (over z), leaf: 64 (over x, y, core).
Axes of the slice: x: 4, y: 8, z: 8, core: 2. Of those that a mesh axis runs over, the one named last changes fastest.
Arguments:
- points: float32 [8, 524288], P(None, ('grp', 'leaf')), may hold values from -6 to 6
- rhs: float32 [16, 524288], P(None, ('grp', 'leaf')), may hold values from -6 to 6
- basis: float32 [524288, 128], P(('grp', 'leaf')), may hold values from -0.1875 to 0.1875
- transfer: float32 [512, 128, 128], P(('grp', 'leaf')), may hold values from -0.5 to 0.5
- noise: float32 [524288], P(('grp', 'leaf')), may hold values from 0.5 to 2
- inv_scale: float32 [8], replicated, may hold values from 0.15 to 0.6
- links: int32 [512, 2], P(('grp', 'leaf')), may hold values from 0 to 1, as said below
- leaf_skel: int32 [512, 128], P(('grp', 'leaf')), may hold values from 0 to 1023, as said below
- group_skel: int32 [8, 128], P('grp'), may hold values from 0 to 8191, as said below
Outputs:
- solution: float32 [16, 524288], P(None, ('grp', 'leaf'))
- residual: float32 [16, 524288], P(None, ('grp', 'leaf'))
Inputs may be any that keep to these rules, and one draw needn't show every extreme that they name: `links`: column 1 of box l equals column 0 of box l + 1; column 0 is 0 for the first box of each group of 64 and column 1 for the last. `leaf_skel`: the 128 indices of a box are distinct. `group_skel`: the 128 indices of a group are distinct.
All inputs are finite; a program needn't handle non-finite values.
Results may differ from a plain program's by a relative error of at most 0.0003.
Values sent between devices are 32-bit elements; how exact they have to be, the bound alone decides.
A program may use at most 128 MiB of HBM per device.

v0:
```python
import functools
import math

import jax
import jax.numpy as jnp
from jax import lax
from jax.experimental import pallas as pl
from jax.experimental.pallas import tpu as pltpu
from jax.sharding import Mesh
from jax.sharding import PartitionSpec as P

GRP_LEAF = ("grp", "leaf_0", "leaf_1", "leaf_2")
MESH = pl.DeviceIdType.MESH
F32 = jnp.float32
BF16 = jnp.bfloat16
FEATURES = 64
LN2 = math.log(2.0)
STRETCH = math.sqrt(5.0) / LN2


def row_of(shape):
    return lax.broadcasted_iota(jnp.int32, shape, 0)


def lane_of(shape):
    return lax.broadcasted_iota(jnp.int32, shape, 1)


def two_parts(value):
    high = value.astype(BF16)
    return high, (value - high.astype(F32)).astype(BF16)


def three_parts(value):
    first = value.astype(BF16).astype(F32)
    rest = value - first
    second = rest.astype(BF16).astype(F32)
    return first, second, (rest - second).astype(BF16).astype(F32)


def features(points, left):
    high, mid, low = three_parts(points)
    norm = jnp.sum(points * points, axis=0, keepdims=True)
    n_high, n_mid, n_low = three_parts(norm)
    row = row_of(points.shape)
    base = 0 if left else 3
    ones = (row >= 3) & (row < 6) if left else row < 3
    norms = jnp.where(
        row == base,
        n_high,
        jnp.where(
            row == base + 1, n_mid, jnp.where(row == base + 2, n_low, jnp.where(ones, 1.0, 0.0))
        ),
    )
    if left:
        two_high, two_mid, two_low = -2.0 * high, -2.0 * mid, -2.0 * low
        pieces = [two_high, two_high, two_mid, two_mid, two_high, two_low]
    else:
        pieces = [high, mid, high, mid, low, high]
    return jnp.concatenate(pieces + [norms, jnp.zeros_like(norms)], axis=0)


def kernel_values(left, right):
    dist = jnp.maximum(jnp.dot(left, right, preferred_element_type=F32), 1e-30)
    scaled = dist * lax.rsqrt(dist)
    return (1.0 + scaled * (LN2 + scaled * (LN2 * LN2 / 3.0))) * jnp.exp2(-scaled)


def fill_block(left_ref, right_ref, high_ref, low_ref):
    rows, columns = high_ref.shape
    tall, wide = min(64, rows), min(256, columns)

    def one(index, carry):
        at = pl.ds(pl.multiple_of(index * tall, tall), tall)
        left = left_ref[at, :]
        for start in range(0, columns, wide):
            values = kernel_values(left, right_ref[:, start : start + wide])
            high, low = two_parts(values)
            high_ref[at, start : start + wide] = high
            low_ref[at, start : start + wide] = low
        return carry

    lax.fori_loop(0, rows // tall, one, 0)


def times(first, second, turned=False):
    dims = (((1,), (1 if turned else 0,)), ((), ()))
    return lax.dot_general(first, second, dims, preferred_element_type=F32)


def product(vec, high, low, turned=False):
    vec_high, vec_low = two_parts(vec)
    rows = vec.shape[0]
    both = times(jnp.concatenate([vec_high, vec_low], axis=0), high, turned)
    return both[:rows] + (both[rows:] + times(vec_high, low, turned))


def side_by_side(buffer, count, start, stop):
    return jnp.concatenate([buffer[slot, start:stop, :] for slot in range(count)], axis=1)


def added_up(buffer, count, start, stop):
    total = buffer[0, start:stop, :]
    for slot in range(1, count):
        total = total + buffer[slot, start:stop, :]
    return total


def lane_sum(value):
    width = value.shape[1]
    total = value[:, :128]
    for start in range(128, width, 128):
        total = total + value[:, start : start + 128]
    return jnp.sum(total, axis=1, keepdims=True)


def everything(
    sizes,
    points_ref,
    rhs_ref,
    basis_ref,
    lift_ref,
    noise_ref,
    leaf_skel_ref,
    group_skel_ref,
    scale_ref,
    links_ref,
    solution_ref,
    residual_ref,
    left_ref,
    right_ref,
    self_high,
    self_low,
    link_high,
    link_low,
    far_high,
    far_low,
    top_high,
    top_low,
    basis_high,
    basis_low,
    lift_high,
    lift_low,
    image_ref,
    points_up,
    vec_up,
    product_out,
    product_in,
    line_1,
    cross_1,
    line_2,
    cross_2_out,
    cross_2_in,
    top_3,
    line_1b,
    cross_1b,
    line_2b,
    cross_2b_out,
    cross_2b_in,
    top_3b,
    sums_1,
    sums_2,
    sums_3,
    send_sem,
    recv_sem,
):
    groups, n_x, n_y, n_core = sizes
    n_cross = n_x * n_core
    boxes = n_cross * n_y
    grp, pos_x, pos_y, pos_core = (lax.axis_index(name) for name in GRP_LEAF)
    box = (pos_x * n_y + pos_y) * n_core + pos_core
    cross = pos_x * n_core + pos_core

    def along_line(step):
        return (grp, pos_x, lax.rem(pos_y + step + n_y, n_y), pos_core)

    def along_cross(step):
        other = lax.rem(cross + step + n_cross, n_cross)
        return (grp, other // n_core, pos_y, lax.rem(other, n_core))

    def along_groups(step):
        return (lax.rem(grp + step + groups, groups), pos_x, pos_y, pos_core)

    def along_boxes(step):
        other = lax.rem(box + step + boxes, boxes)
        return (
            grp,
            other // (n_y * n_core),
            lax.rem(other // n_core, n_y),
            lax.rem(other, n_core),
        )

    barrier = pltpu.get_barrier_semaphore()
    partners = [along_line(step) for step in range(1, n_y)]
    partners += [along_cross(step) for step in range(1, n_cross)]
    partners += [along_groups(step) for step in range(1, groups)]
    partners += [along_boxes(-1), along_boxes(1)]
    for partner in partners:
        pl.semaphore_signal(barrier, inc=1, device_id=partner, device_id_type=MESH)

    started = []

    def send(source, target, device):
        index = len(started)
        copy = pltpu.make_async_remote_copy(
            src_ref=source,
            dst_ref=target,
            send_sem=send_sem.at[index],
            recv_sem=recv_sem.at[index],
            device_id=device,
            device_id_type=MESH,
        )
        copy.start()
        started.append(copy)
        return copy

    def spread(buffer, count, along):
        order = sorted(range(1, count), key=lambda step: -min(step, count - step))
        return [send(buffer.at[0], buffer.at[step], along(step)) for step in order]

    def arrived(copies):
        for copy in copies:
            copy.wait_recv()

    inv_column = jnp.zeros((8, 1), F32)
    for dim in range(8):
        inv_column = jnp.where(row_of((8, 1)) == dim, scale_ref[dim], inv_column)
    inv_column = inv_column * STRETCH
    left_bit = links_ref[0, 0].astype(F32)
    right_bit = links_ref[0, 1].astype(F32)
    weight_self = 1.0 + left_bit + right_bit

    basis_high[...], basis_low[...] = two_parts(basis_ref[...])
    lift_high[...], lift_low[...] = two_parts(lift_ref[0])
    rhs = rhs_ref[...]
    coeff = product(rhs, basis_high[...], basis_low[...])
    lifted = product(coeff, lift_high[...], lift_low[...])
    own = points_ref[...] * inv_column
    width = own.shape[1]
    picked = jnp.where(row_of((width, 128)) == leaf_skel_ref[...], 1.0, 0.0).astype(BF16)
    parts = times(jnp.concatenate(three_parts(own), axis=0).astype(BF16), picked)
    skel = parts[:8] + (parts[8:16] + parts[16:])
    held = jnp.where(row_of((128, 128)) == group_skel_ref[...] - box * 128, 1.0, 0.0).astype(BF16)
    parts = times(jnp.concatenate(three_parts(skel), axis=0).astype(BF16), held)
    top_part = parts[:8] + (parts[8:16] + parts[16:])
    line_1[0, :16, :] = coeff
    line_1[0, 16:, :] = skel
    cross_1[0, :16, :] = lifted
    cross_1[0, 16:24, :] = skel
    cross_1[0, 24:, :] = top_part

    pl.semaphore_wait(barrier, len(partners))
    cross_1_copies = spread(cross_1, n_cross, along_cross)
    line_1_copies = spread(line_1, n_y, along_line)
    points_copy = send(points_ref, points_up, along_boxes(-1))
    vec_copy = send(rhs_ref, vec_up.at[0], along_boxes(-1))

    left_ref[...] = features(own, True).T.astype(BF16)
    right_ref[...] = features(own, False).astype(BF16)
    fill_block(left_ref, right_ref, self_high, self_low)

    arrived(cross_1_copies)
    line_2[0, :16, :] = added_up(cross_1, n_cross, 0, 16)
    line_2[0, 16:, :] = added_up(cross_1, n_cross, 24, 32)
    line_2_copies = spread(line_2, n_y, along_line)

    arrived([points_copy, vec_copy])
    right_ref[...] = features(points_up[...] * inv_column, False).astype(BF16)
    fill_block(left_ref, right_ref, link_high, link_low)
    product_out[0] = right_bit * product(rhs, link_high[...], link_low[...])
    product_copy = send(product_out.at[0], product_in.at[0], along_boxes(1))

    arrived(line_1_copies)
    far_left = features(side_by_side(line_1, n_y, 16, 24), True).T
    left_ref[: n_y * 128, :] = far_left.astype(BF16)
    far_right = features(side_by_side(cross_1, n_cross, 16, 24), False)
    right_ref[:, : n_cross * 128] = far_right.astype(BF16)
    fill_block(left_ref, right_ref, far_high, far_low)

    arrived(line_2_copies)
    top_3[0, :16, :] = added_up(line_2, n_y, 0, 16)
    top_own = added_up(line_2, n_y, 16, 24)
    top_3[0, 16:, :] = top_own
    top_3_copies = spread(top_3, groups, along_groups)

    def far_terms(coeffs, out, into):
        spread_out = product(coeffs, far_high[...], far_low[...])
        out[0] = spread_out[:, :128]
        copies = []
        for slot in range(1, n_cross):
            out[slot] = spread_out[:, slot * 128 : (slot + 1) * 128]
        order = sorted(range(1, n_cross), key=lambda step: -min(step, n_cross - step))
        for slot in order:
            copies.append(send(out.at[slot], into.at[slot], along_cross(-slot)))
        return copies

    def far_sum(out, into):
        total = out[0]
        for slot in range(1, n_cross):
            total = total + into[slot]
        return total

    cross_2_copies = far_terms(side_by_side(line_1, n_y, 0, 16), cross_2_out, cross_2_in)

    noise = noise_ref[...]

    def near_part(vec, above):
        return (
            noise * vec
            + weight_self * product(vec, self_high[...], self_low[...])
            + right_bit * product(above, link_high[...], link_low[...], True)
        )

    def rest(far, top_coeff):
        top = product(top_coeff, top_high[...], top_low[...])
        row = far + product(top, lift_high[...], lift_low[...], True)
        return product(row, basis_high[...], basis_low[...], True)

    near = near_part(rhs, vec_up[0])
    dot_rr = lane_sum(rhs * rhs)

    arrived(cross_2_copies)
    far = far_sum(cross_2_out, cross_2_in)
    arrived(top_3_copies)
    top_left = features(side_by_side(top_3, groups, 16, 24), True).T
    left_ref[: groups * 128, :] = top_left.astype(BF16)
    right_ref[:, :128] = features(top_own, False).astype(BF16)
    fill_block(left_ref, right_ref.at[:, :128], top_high, top_low)
    image = near + rest(far, side_by_side(top_3, groups, 0, 16))
    arrived([product_copy])
    image = image + product_in[0]
    image_ref[...] = image

    coeff = product(image, basis_high[...], basis_low[...])
    line_1b[0] = coeff
    line_1b_copies = spread(line_1b, n_y, along_line)
    cross_1b[0] = product(coeff, lift_high[...], lift_low[...])
    cross_1b_copies = spread(cross_1b, n_cross, along_cross)
    vec_copy = send(image_ref, vec_up.at[1], along_boxes(-1))
    product_out[1] = right_bit * product(image, link_high[...], link_low[...])
    product_copy = send(product_out.at[1], product_in.at[1], along_boxes(1))
    arrived(cross_1b_copies)
    line_2b[0] = added_up(cross_1b, n_cross, 0, 16)
    line_2b_copies = spread(line_2b, n_y, along_line)
    arrived(line_1b_copies)
    cross_2b_copies = far_terms(side_by_side(line_1b, n_y, 0, 16), cross_2b_out, cross_2b_in)
    arrived([vec_copy])
    near = near_part(image, vec_up[1])
    arrived(line_2b_copies)
    top_3b[0] = added_up(line_2b, n_y, 0, 16)
    top_3b_copies = spread(top_3b, groups, along_groups)
    dot_rw = lane_sum(rhs * image)
    dot_ww = lane_sum(image * image)
    arrived([product_copy])
    near = near + product_in[1]
    arrived(cross_2b_copies)
    far = far_sum(cross_2b_out, cross_2b_in)
    arrived(top_3b_copies)
    second = near + rest(far, side_by_side(top_3b, groups, 0, 16))
    dot_wu = lane_sum(image * second)

    lane = lane_of((8, 128))
    packed = jnp.zeros((8, 128), F32)
    for index, dot in enumerate((dot_rr, dot_rw, dot_ww, dot_wu)):
        packed = jnp.where(lane == index, dot[:8], packed)
        packed = jnp.where(lane == index + 4, dot[8:], packed)
    sums_1[0] = packed
    arrived(spread(sums_1, n_y, along_line))
    sums_2[0] = added_up(sums_1, n_y, 0, 8)
    arrived(spread(sums_2, n_cross, along_cross))
    sums_3[0] = added_up(sums_2, n_cross, 0, 8)
    arrived(spread(sums_3, groups, along_groups))
    total = added_up(sums_3, groups, 0, 8)
    rr, rw, ww, wu = (
        jnp.concatenate([total[:, index : index + 1], total[:, index + 4 : index + 5]], axis=0)
        for index in range(4)
    )

    alpha = rr / rw
    next_rr = rr - 2.0 * alpha * rw + alpha * alpha * ww
    curve = rw - 2.0 * alpha * ww + alpha * alpha * wu
    ratio = next_rr / rr
    next_alpha = next_rr / (curve - ratio * next_rr / alpha)
    one = alpha + next_alpha * (1.0 + ratio)
    two = alpha * next_alpha
    solution_ref[...] = one * rhs - two * image
    residual_ref[...] = rhs - one * image + two * second

    for copy in started:
        copy.wait_send()


def copies_of(sizes):
    groups, n_x, n_y, n_core = sizes
    n_cross = n_x * n_core
    return 5 * (n_y - 1) + 5 * (n_cross - 1) + 3 * (groups - 1) + 5


def local(sizes, points, rhs, basis, transfer, noise, inv_scale, links, leaf_skel, group_skel):
    groups, n_x, n_y, n_core = sizes
    n_cross = n_x * n_core
    width = points.shape[1]
    rows = rhs.shape[0]
    skel = leaf_skel.shape[1]
    vmem = pl.BlockSpec(memory_space=pltpu.VMEM)
    smem = pl.BlockSpec(memory_space=pltpu.SMEM)
    count = copies_of(sizes)

    def held(*shape):
        return pltpu.VMEM(shape, F32)

    def halves(*shape):
        return [pltpu.VMEM(shape, BF16)] * 2

    scratch = [
        pltpu.VMEM((width, FEATURES), BF16),
        pltpu.VMEM((FEATURES, width), BF16),
        *halves(width, width),
        *halves(width, width),
        *halves(n_y * skel, n_cross * skel),
        *halves(groups * skel, skel),
        *halves(width, skel),
        *halves(skel, skel),
        held(rows, width),
        held(8, width),
        held(2, rows, width),
        held(2, rows, width),
        held(2, rows, width),
        held(n_y, rows + 8, skel),
        held(n_cross, rows + 16, skel),
        held(n_y, rows + 8, skel),
        held(n_cross, rows, skel),
        held(n_cross, rows, skel),
        held(groups, rows + 8, skel),
        held(n_y, rows, skel),
        held(n_cross, rows, skel),
        held(n_y, rows, skel),
        held(n_cross, rows, skel),
        held(n_cross, rows, skel),
        held(groups, rows, skel),
        held(n_y, 8, skel),
        held(n_cross, 8, skel),
        held(groups, 8, skel),
        pltpu.SemaphoreType.DMA((count,)),
        pltpu.SemaphoreType.DMA((count,)),
    ]
    return pl.pallas_call(
        functools.partial(everything, sizes),
        name="skeleton_cg",
        out_shape=(jax.ShapeDtypeStruct(rhs.shape, F32), jax.ShapeDtypeStruct(rhs.shape, F32)),
        in_specs=[vmem, vmem, vmem, vmem, vmem, vmem, vmem, smem, smem],
        out_specs=(vmem, vmem),
        scratch_shapes=scratch,
        compiler_params=pltpu.CompilerParams(
            collective_id=0, has_side_effects=True, vmem_limit_bytes=48 * 1024 * 1024
        ),
    )(
        points,
        rhs,
        basis,
        transfer,
        noise[None, :],
        leaf_skel,
        group_skel,
        inv_scale,
        links,
    )


def on_finer(finer):
    placed = (
        P(None, GRP_LEAF),
        P(None, GRP_LEAF),
        P(GRP_LEAF, None),
        P(GRP_LEAF, None, None),
        P(GRP_LEAF),
        P(),
        P(GRP_LEAF, None),
        P(GRP_LEAF, None),
        P("grp", None),
    )
    sizes = tuple(finer.shape[name] for name in GRP_LEAF)
    return jax.shard_map(
        functools.partial(local, sizes),
        mesh=finer,
        in_specs=placed,
        out_specs=(P(None, GRP_LEAF), P(None, GRP_LEAF)),
        check_vma=False,
    )


def solution(mesh):
    finer = Mesh(mesh.devices.reshape(mesh.shape["grp"], 4, 8, 2), GRP_LEAF)
    return on_finer(finer)
```

profile of v0, /device:TPU:1, one launch (start us, length us, event | category | flops | bytes accessed | tf_op | source)
XLA Modules:
  0.0 73.7 jit_solution(6694357096313630192)
XLA Ops:
  0.6 0.0 copy-start.6
  0.6 0.0 copy-start.5
  0.7 0.0 copy-start.7
  0.7 0.6 copy-done.6
  1.3 0.0 copy-done.5
  1.3 0.0 copy-done.7
  1.3 0.0 copy-start
  1.3 1.0 %copy-done = f32[1024,128]{1,0:T(8,128)S(1)} copy-done((f32[1024,128]{1,0:T(8,128)S(1)}, f32[1024,128]{1,0:T(8,128)}, u32[]{:S(2)}) %copy-start) | copy-done | bytes 524312
  2.4 0.0 copy-start.1
  2.4 0.8 %copy-done.1 = f32[16,1024]{1,0:T(8,128)S(1)} copy-done((f32[16,1024]{1,0:T(8,128)S(1)}, f32[16,1024]{1,0:T(8,128)}, u32[]{:S(2)}) %copy-start.1) | copy-done | bytes 65560
  3.2 0.0 copy-start.2
  3.2 0.8 %copy-done.2 = f32[1,128,128]{2,1,0:T(8,128)S(1)} copy-done((f32[1,128,128]{2,1,0:T(8,128)S(1)}, f32[1,128,128]{2,1,0:T(8,128)}, u32[]{:S(2)}) %copy-start.2) | copy-done | bytes 65560
  4.0 0.0 copy-start.3
  4.0 0.8 %copy-done.3 = f32[8,1024]{1,0:T(8,128)S(1)} copy-done((f32[8,1024]{1,0:T(8,128)S(1)}, f32[8,1024]{1,0:T(8,128)}, u32[]{:S(2)}) %copy-start.3) | copy-done | bytes 32792
  4.8 0.0 copy-start.4
  4.8 0.7 copy-done.4
  5.5 0.0 copy-start.8
  5.5 0.7 copy-done.8
  6.1 66.2 %skeleton_cg.1 = (f32[16,1024]{1,0:T(8,128)S(1)}, f32[16,1024]{1,0:T(8,128)S(1)}) custom-call(f32[8,1024]{1,0:T(8,128)S(1)} %copy-done.3, f32[16,1024]{1,0:T(8,128)S(1)} %copy-done.1, f32[1024,128]{1,0:T(8,128)S(1)} %copy-done, f32[1,128,128]{2,1,0:T(8,128)S(1)} %copy-done.2, f32[1,1024]{1,0:T(1,128)S(1)} %bitcast.1, s32[1,128]{1,0:T(1,128)S(1)} %copy-done.5, ...), custom_call_target="tpu_custom_call" | custom-call | tf_op jit(solution)/shard_map/skeleton_cg/pallas_call | solution.py:447
  72.4 0.6 copy.13
  73.0 0.6 copy.14
Async XLA Ops:
  0.6 0.7 copy-start.6
  0.6 0.7 copy-start.5
  0.7 0.7 copy-start.7
  1.3 1.0 %copy-start = (f32[1024,128]{1,0:T(8,128)S(1)}, f32[1024,128]{1,0:T(8,128)}, u32[]{:S(2)}) copy-start(f32[1024,128]{1,0:T(8,128)} %basis_ref.1) | copy-start | bytes 1572868
  2.4 0.8 %copy-start.1 = (f32[16,1024]{1,0:T(8,128)S(1)}, f32[16,1024]{1,0:T(8,128)}, u32[]{:S(2)}) copy-start(f32[16,1024]{1,0:T(8,128)} %rhs_ref.1) | copy-start | bytes 196612
  3.2 0.8 %copy-start.2 = (f32[1,128,128]{2,1,0:T(8,128)S(1)}, f32[1,128,128]{2,1,0:T(8,128)}, u32[]{:S(2)}) copy-start(f32[1,128,128]{2,1,0:T(8,128)} %lift_ref.1) | copy-start | bytes 196612
  4.0 0.8 %copy-start.3 = (f32[8,1024]{1,0:T(8,128)S(1)}, f32[8,1024]{1,0:T(8,128)}, u32[]{:S(2)}) copy-start(f32[8,1024]{1,0:T(8,128)} %points_ref.1) | copy-start | bytes 98308
  4.8 0.7 copy-start.4
  5.5 0.7 copy-start.8
where the time goes:
time: 74 us; the launch traced here: 73.7 us
  Pallas kernels  66.2 us (89%)
  local copies, waits for them, and re-layouts  6.74 us (9%)
    pallas_call x1, Pallas kernels, local(): pl.pallas_call(functools.partial(everything, sizes), name='skeleton_cg',...  66.2 us
    unnamed x20, local copies, waits for them, and re-layouts  6.74 us

commit v1 on v0

--- a/solution.py
+++ b/solution.py
@@ -66,18 +66,21 @@
     return (1.0 + scaled * (LN2 + scaled * (LN2 * LN2 / 3.0))) * jnp.exp2(-scaled)
 
 
-def fill_block(left_ref, right_ref, high_ref, low_ref):
+def fill_block(left_ref, right_ref, high_ref, low_ref, first=0, last=None):
     rows, columns = high_ref.shape
-    tall, wide = min(64, rows), min(256, columns)
+    last = columns if last is None else last
+    wide = min(256, last - first)
+    tall = min(rows, 64 if last - first > 256 else 256)
 
     def one(index, carry):
         at = pl.ds(pl.multiple_of(index * tall, tall), tall)
         left = left_ref[at, :]
-        for start in range(0, columns, wide):
-            values = kernel_values(left, right_ref[:, start : start + wide])
+        for start in range(first, last, wide):
+            stop = min(start + wide, last)
+            values = kernel_values(left, right_ref[:, start:stop])
             high, low = two_parts(values)
-            high_ref[at, start : start + wide] = high
-            low_ref[at, start : start + wide] = low
+            high_ref[at, start:stop] = high
+            low_ref[at, start:stop] = low
         return carry
 
     lax.fori_loop(0, rows // tall, one, 0)
@@ -116,19 +119,32 @@
 
 def everything(
     sizes,
+    points_hbm,
+    rhs_hbm,
+    basis_hbm,
+    lift_hbm,
+    noise_hbm,
+    scale_hbm,
+    links_hbm,
+    leaf_skel_hbm,
+    group_skel_hbm,
+    image_ref,
+    second_ref,
+    one_ref,
+    two_ref,
     points_ref,
     rhs_ref,
     basis_ref,
     lift_ref,
     noise_ref,
+    scale_ref,
+    links_ref,
     leaf_skel_ref,
     group_skel_ref,
-    scale_ref,
-    links_ref,
-    solution_ref,
-    residual_ref,
     left_ref,
     right_ref,
+    top_left_ref,
+    top_right_ref,
     self_high,
     self_low,
     link_high,
@@ -139,9 +155,16 @@
     top_low,
     basis_high,
     basis_low,
+    turned_high,
+    turned_low,
     lift_high,
     lift_low,
-    image_ref,
+    lower_high,
+    lower_low,
+    gram_high,
+    gram_low,
+    jump_high,
+    jump_low,
     points_up,
     vec_up,
     product_out,
@@ -161,6 +184,7 @@
     sums_1,
     sums_2,
     sums_3,
+    load_sem,
     send_sem,
     recv_sem,
 ):
@@ -190,10 +214,27 @@
             lax.rem(other, n_core),
         )
 
+    loads = {}
+    for index, (name, source, target) in enumerate(
+        (
+            ("rhs", rhs_hbm, rhs_ref),
+            ("basis", basis_hbm, basis_ref),
+            ("lift", lift_hbm, lift_ref),
+            ("points", points_hbm, points_ref),
+            ("scale", scale_hbm, scale_ref),
+            ("leaf_skel", leaf_skel_hbm, leaf_skel_ref),
+            ("group_skel", group_skel_hbm, group_skel_ref),
+            ("links", links_hbm, links_ref),
+            ("noise", noise_hbm, noise_ref),
+        )
+    ):
+        loads[name] = pltpu.make_async_copy(source, target, load_sem.at[index])
+        loads[name].start()
+
     barrier = pltpu.get_barrier_semaphore()
-    partners = [along_line(step) for step in range(1, n_y)]
+    partners = [along_groups(step) for step in range(1, groups)]
+    partners += [along_line(step) for step in range(1, n_y)]
     partners += [along_cross(step) for step in range(1, n_cross)]
-    partners += [along_groups(step) for step in range(1, groups)]
     partners += [along_boxes(-1), along_boxes(1)]
     for partner in partners:
         pl.semaphore_signal(barrier, inc=1, device_id=partner, device_id_type=MESH)
@@ -222,19 +263,23 @@
         for copy in copies:
             copy.wait_recv()
 
-    inv_column = jnp.zeros((8, 1), F32)
-    for dim in range(8):
-        inv_column = jnp.where(row_of((8, 1)) == dim, scale_ref[dim], inv_column)
-    inv_column = inv_column * STRETCH
-    left_bit = links_ref[0, 0].astype(F32)
-    right_bit = links_ref[0, 1].astype(F32)
-    weight_self = 1.0 + left_bit + right_bit
-
-    basis_high[...], basis_low[...] = two_parts(basis_ref[...])
-    lift_high[...], lift_low[...] = two_parts(lift_ref[0])
+    def keep(value, high_ref, low_ref):
+        high_ref[...], low_ref[...] = two_parts(value)
+
+    loads["rhs"].wait()
+    loads["basis"].wait()
     rhs = rhs_ref[...]
+    keep(basis_ref[...], basis_high, basis_low)
     coeff = product(rhs, basis_high[...], basis_low[...])
+    loads["lift"].wait()
+    keep(lift_ref[0], lift_high, lift_low)
     lifted = product(coeff, lift_high[...], lift_low[...])
+    loads["points"].wait()
+    loads["scale"].wait()
+    loads["leaf_skel"].wait()
+    loads["group_skel"].wait()
+    diagonal = row_of((8, 8)) == lane_of((8, 8))
+    inv_column = jnp.sum(jnp.where(diagonal, scale_ref[...], 0.0), axis=1, keepdims=True) * STRETCH
     own = points_ref[...] * inv_column
     width = own.shape[1]
     picked = jnp.where(row_of((width, 128)) == leaf_skel_ref[...], 1.0, 0.0).astype(BF16)
@@ -243,11 +288,11 @@
     held = jnp.where(row_of((128, 128)) == group_skel_ref[...] - box * 128, 1.0, 0.0).astype(BF16)
     parts = times(jnp.concatenate(three_parts(skel), axis=0).astype(BF16), held)
     top_part = parts[:8] + (parts[8:16] + parts[16:])
-    line_1[0, :16, :] = coeff
-    line_1[0, 16:, :] = skel
     cross_1[0, :16, :] = lifted
     cross_1[0, 16:24, :] = skel
     cross_1[0, 24:, :] = top_part
+    line_1[0, :16, :] = coeff
+    line_1[0, 16:, :] = skel
 
     pl.semaphore_wait(barrier, len(partners))
     cross_1_copies = spread(cross_1, n_cross, along_cross)
@@ -255,6 +300,10 @@
     points_copy = send(points_ref, points_up, along_boxes(-1))
     vec_copy = send(rhs_ref, vec_up.at[0], along_boxes(-1))
 
+    loads["links"].wait()
+    loads["noise"].wait()
+    right_bit = links_ref[:, 1:2].astype(F32)
+    weight_self = 1.0 + links_ref[:, 0:1].astype(F32) + right_bit
     left_ref[...] = features(own, True).T.astype(BF16)
     right_ref[...] = features(own, False).astype(BF16)
     fill_block(left_ref, right_ref, self_high, self_low)
@@ -283,16 +332,11 @@
     top_3[0, 16:, :] = top_own
     top_3_copies = spread(top_3, groups, along_groups)
 
-    def far_terms(coeffs, out, into):
-        spread_out = product(coeffs, far_high[...], far_low[...])
-        out[0] = spread_out[:, :128]
-        copies = []
-        for slot in range(1, n_cross):
+    def far_terms(spread_out, out, into):
+        for slot in range(n_cross):
             out[slot] = spread_out[:, slot * 128 : (slot + 1) * 128]
         order = sorted(range(1, n_cross), key=lambda step: -min(step, n_cross - step))
-        for slot in order:
-            copies.append(send(out.at[slot], into.at[slot], along_cross(-slot)))
-        return copies
+        return [send(out.at[slot], into.at[slot], along_cross(-slot)) for slot in order]
 
     def far_sum(out, into):
         total = out[0]
@@ -300,64 +344,76 @@
             total = total + into[slot]
         return total
 
-    cross_2_copies = far_terms(side_by_side(line_1, n_y, 0, 16), cross_2_out, cross_2_in)
+    line_coeff = side_by_side(line_1, n_y, 0, 16)
+    cross_2_copies = far_terms(
+        product(line_coeff, far_high[...], far_low[...]), cross_2_out, cross_2_in
+    )
 
     noise = noise_ref[...]
 
-    def near_part(vec, above):
-        return (
-            noise * vec
-            + weight_self * product(vec, self_high[...], self_low[...])
-            + right_bit * product(above, link_high[...], link_low[...], True)
-        )
-
-    def rest(far, top_coeff):
-        top = product(top_coeff, top_high[...], top_low[...])
-        row = far + product(top, lift_high[...], lift_low[...], True)
-        return product(row, basis_high[...], basis_low[...], True)
-
-    near = near_part(rhs, vec_up[0])
+    def self_part(vec):
+        return noise * vec + weight_self * product(vec, self_high[...], self_low[...])
+
+    def upper_part(above):
+        return right_bit * product(above, link_high[...], link_low[...], True)
+
+    near = self_part(rhs) + upper_part(vec_up[0])
+
+    turned = basis_ref[...].T
+    keep(turned, turned_high, turned_low)
+    gram = product(turned, basis_high[...], basis_low[...])
+    both = jnp.concatenate([gram, product(gram, lift_high[...], lift_low[...])], axis=1)
+    keep(both, gram_high, gram_low)
+    lower = lift_ref[0].T
+    keep(lower, lower_high, lower_low)
+    keep(product(lower, gram_high[...], gram_low[...]), jump_high, jump_low)
     dot_rr = lane_sum(rhs * rhs)
 
+    arrived([product_copy])
+    near = near + product_in[0]
+    image_ref[...] = near
+    near_coeff = product(near, basis_high[...], basis_low[...])
+    known = jnp.concatenate(
+        [near_coeff, product(near_coeff, lift_high[...], lift_low[...])], axis=1
+    )
     arrived(cross_2_copies)
     far = far_sum(cross_2_out, cross_2_in)
+    known = known + product(far, gram_high[...], gram_low[...])
+    top_right_ref[:, :128] = features(top_own, False).astype(BF16)
+
     arrived(top_3_copies)
-    top_left = features(side_by_side(top_3, groups, 16, 24), True).T
-    left_ref[: groups * 128, :] = top_left.astype(BF16)
-    right_ref[:, :128] = features(top_own, False).astype(BF16)
-    fill_block(left_ref, right_ref.at[:, :128], top_high, top_low)
-    image = near + rest(far, side_by_side(top_3, groups, 0, 16))
-    arrived([product_copy])
-    image = image + product_in[0]
-    image_ref[...] = image
-
-    coeff = product(image, basis_high[...], basis_low[...])
+    top_all = side_by_side(top_3, groups, 16, 24)
+    top_left_ref[...] = features(top_all, True).T.astype(BF16)
+    fill_block(top_left_ref, top_right_ref, top_high, top_low, 0, 128)
+    top = product(side_by_side(top_3, groups, 0, 16), top_high[:, :128], top_low[:, :128])
+    both = known + product(top, jump_high[...], jump_low[...])
+    coeff = both[:, :128]
+    cross_1b[0, :16, :] = both[:, 128:]
+    cross_1b[0, 16:, :] = coeff
     line_1b[0] = coeff
     line_1b_copies = spread(line_1b, n_y, along_line)
-    cross_1b[0] = product(coeff, lift_high[...], lift_low[...])
     cross_1b_copies = spread(cross_1b, n_cross, along_cross)
+    row = far + product(top, lower_high[...], lower_low[...])
+    image = image_ref[...] + product(row, turned_high[...], turned_low[...])
+    image_ref[...] = image
     vec_copy = send(image_ref, vec_up.at[1], along_boxes(-1))
     product_out[1] = right_bit * product(image, link_high[...], link_low[...])
     product_copy = send(product_out.at[1], product_in.at[1], along_boxes(1))
+    near = self_part(image)
+    dot_rw = lane_sum(rhs * image)
+    dot_ww = lane_sum(image * image)
+    dot_wu = lane_sum(image * near)
     arrived(cross_1b_copies)
     line_2b[0] = added_up(cross_1b, n_cross, 0, 16)
     line_2b_copies = spread(line_2b, n_y, along_line)
+    arrived([vec_copy])
+    upper = upper_part(vec_up[1])
+    dot_wu = dot_wu + 2.0 * lane_sum(image * upper)
+    second_ref[...] = near + upper
     arrived(line_1b_copies)
-    cross_2b_copies = far_terms(side_by_side(line_1b, n_y, 0, 16), cross_2b_out, cross_2b_in)
-    arrived([vec_copy])
-    near = near_part(image, vec_up[1])
-    arrived(line_2b_copies)
-    top_3b[0] = added_up(line_2b, n_y, 0, 16)
-    top_3b_copies = spread(top_3b, groups, along_groups)
-    dot_rw = lane_sum(rhs * image)
-    dot_ww = lane_sum(image * image)
-    arrived([product_copy])
-    near = near + product_in[1]
-    arrived(cross_2b_copies)
-    far = far_sum(cross_2b_out, cross_2b_in)
-    arrived(top_3b_copies)
-    second = near + rest(far, side_by_side(top_3b, groups, 0, 16))
-    dot_wu = lane_sum(image * second)
+    spread_out = product(side_by_side(line_1b, n_y, 0, 16), far_high[...], far_low[...])
+    cross_2b_copies = far_terms(spread_out, cross_2b_out, cross_2b_in)
+    dot_wu = dot_wu + lane_sum(spread_out * side_by_side(cross_1b, n_cross, 16, 32))
 
     lane = lane_of((8, 128))
     packed = jnp.zeros((8, 128), F32)
@@ -365,26 +421,46 @@
         packed = jnp.where(lane == index, dot[:8], packed)
         packed = jnp.where(lane == index + 4, dot[8:], packed)
     sums_1[0] = packed
-    arrived(spread(sums_1, n_y, along_line))
-    sums_2[0] = added_up(sums_1, n_y, 0, 8)
-    arrived(spread(sums_2, n_cross, along_cross))
-    sums_3[0] = added_up(sums_2, n_cross, 0, 8)
-    arrived(spread(sums_3, groups, along_groups))
+    sums_1_copies = spread(sums_1, n_cross, along_cross)
+
+    top_right_ref[...] = features(top_all, False).astype(BF16)
+    fill_block(top_left_ref, top_right_ref, top_high, top_low, 128)
+
+    arrived(line_2b_copies)
+    top_3b[0] = added_up(line_2b, n_y, 0, 16)
+    top_3b_copies = spread(top_3b, groups, along_groups)
+    arrived(sums_1_copies)
+    sums_2[0] = added_up(sums_1, n_cross, 0, 8)
+    sums_2_copies = spread(sums_2, n_y, along_line)
+    arrived([product_copy])
+    arrived(cross_2b_copies)
+    far = far_sum(cross_2b_out, cross_2b_in)
+    arrived(sums_2_copies)
+    sums_3[0] = added_up(sums_2, n_y, 0, 8)
+    sums_3_copies = spread(sums_3, groups, along_groups)
+    arrived(top_3b_copies)
+    top_coeff = side_by_side(top_3b, groups, 0, 16)
+    top_out = product(top_coeff, top_high[...], top_low[...])
+    row = far + product(top_out[:, :128], lower_high[...], lower_low[...])
+    second_ref[...] = (
+        second_ref[...] + product_in[1] + product(row, turned_high[...], turned_low[...])
+    )
+    top_wu = lane_sum(top_out * top_coeff)
+    arrived(sums_3_copies)
     total = added_up(sums_3, groups, 0, 8)
     rr, rw, ww, wu = (
         jnp.concatenate([total[:, index : index + 1], total[:, index + 4 : index + 5]], axis=0)
         for index in range(4)
     )
+    wu = wu + top_wu
 
     alpha = rr / rw
     next_rr = rr - 2.0 * alpha * rw + alpha * alpha * ww
     curve = rw - 2.0 * alpha * ww + alpha * alpha * wu
     ratio = next_rr / rr
     next_alpha = next_rr / (curve - ratio * next_rr / alpha)
-    one = alpha + next_alpha * (1.0 + ratio)
-    two = alpha * next_alpha
-    solution_ref[...] = one * rhs - two * image
-    residual_ref[...] = rhs - one * image + two * second
+    one_ref[...] = jnp.broadcast_to(alpha + next_alpha * (1.0 + ratio), one_ref.shape)
+    two_ref[...] = jnp.broadcast_to(alpha * next_alpha, two_ref.shape)
 
     for copy in started:
         copy.wait_send()
@@ -402,9 +478,18 @@
     width = points.shape[1]
     rows = rhs.shape[0]
     skel = leaf_skel.shape[1]
-    vmem = pl.BlockSpec(memory_space=pltpu.VMEM)
-    smem = pl.BlockSpec(memory_space=pltpu.SMEM)
     count = copies_of(sizes)
+    operands = (
+        points,
+        rhs,
+        basis,
+        transfer,
+        noise[None, :],
+        inv_scale[None, :],
+        links,
+        leaf_skel,
+        group_skel,
+    )
 
     def held(*shape):
         return pltpu.VMEM(shape, F32)
@@ -413,15 +498,21 @@
         return [pltpu.VMEM(shape, BF16)] * 2
 
     scratch = [
+        *[pltpu.VMEM(operand.shape, operand.dtype) for operand in operands],
         pltpu.VMEM((width, FEATURES), BF16),
         pltpu.VMEM((FEATURES, width), BF16),
+        pltpu.VMEM((groups * skel, FEATURES), BF16),
+        pltpu.VMEM((FEATURES, groups * skel), BF16),
         *halves(width, width),
         *halves(width, width),
         *halves(n_y * skel, n_cross * skel),
-        *halves(groups * skel, skel),
+        *halves(groups * skel, groups * skel),
         *halves(width, skel),
+        *halves(skel, width),
         *halves(skel, skel),
-        held(rows, width),
+        *halves(skel, skel),
+        *halves(skel, 2 * skel),
+        *halves(skel, 2 * skel),
         held(8, width),
         held(2, rows, width),
         held(2, rows, width),
@@ -433,38 +524,31 @@
         held(n_cross, rows, skel),
         held(groups, rows + 8, skel),
         held(n_y, rows, skel),
-        held(n_cross, rows, skel),
+        held(n_cross, 2 * rows, skel),
         held(n_y, rows, skel),
         held(n_cross, rows, skel),
         held(n_cross, rows, skel),
         held(groups, rows, skel),
+        held(n_cross, 8, skel),
         held(n_y, 8, skel),
-        held(n_cross, 8, skel),
         held(groups, 8, skel),
+        pltpu.SemaphoreType.DMA((len(operands),)),
         pltpu.SemaphoreType.DMA((count,)),
         pltpu.SemaphoreType.DMA((count,)),
     ]
-    return pl.pallas_call(
+    vmem = pl.BlockSpec(memory_space=pltpu.VMEM)
+    image, second, one, two = pl.pallas_call(
         functools.partial(everything, sizes),
         name="skeleton_cg",
-        out_shape=(jax.ShapeDtypeStruct(rhs.shape, F32), jax.ShapeDtypeStruct(rhs.shape, F32)),
-        in_specs=[vmem, vmem, vmem, vmem, vmem, vmem, vmem, smem, smem],
-        out_specs=(vmem, vmem),
+        out_shape=[jax.ShapeDtypeStruct(rhs.shape, F32)] * 4,
+        in_specs=[pl.BlockSpec(memory_space=pltpu.HBM)] * len(operands),
+        out_specs=[vmem] * 4,
         scratch_shapes=scratch,
         compiler_params=pltpu.CompilerParams(
-            collective_id=0, has_side_effects=True, vmem_limit_bytes=48 * 1024 * 1024
+            collective_id=0, has_side_effects=True
         ),
-    )(
-        points,
-        rhs,
-        basis,
-        transfer,
-        noise[None, :],
-        leaf_skel,
-        group_skel,
-        inv_scale,
-        links,
-    )
+    )(*operands)
+    return one * rhs - two * image, rhs - one * image + two * second
 
 
 def on_finer(finer):

time: 74 us -> 59.2 us (0.80)
  Pallas kernels: 66.2 us -> 56.7 us
  local copies, waits for them, and re-layouts: 6.74 us -> 0.01 us
  other arithmetic: 0 us -> 1.61 us
    pallas_call x1, Pallas kernels: 66.2 us -> 56.7 us  [local(): pl.pallas_call(functools.partial(everything, sizes), name='skeleton_cg',...]
    unnamed x20 -> x2, local copies, waits for them, and re-layouts: 6.74 us -> 0.01 us
    add x0 -> x1, other arithmetic: none -> 1.61 us  [local(): return (one * rhs - two * image, rhs - one * image + two * second)]
where the time goes in v1:
time: 59.2 us; the launch traced here: 59 us
  Pallas kernels  56.7 us (96%)
  other arithmetic  1.61 us (3%)
  between operations  0.66 us (1%)
    pallas_call x1, Pallas kernels, local(): pl.pallas_call(functools.partial(everything, sizes), name='skeleton_cg',...  56.7 us
    add x1, other arithmetic, local(): return (one * rhs - two * image, rhs - one * image + two * second)  1.61 us

profile of v1, /device:TPU:1, one launch (start us, length us, event | category | flops | bytes accessed | tf_op | source)
XLA Modules:
  0.0 59.0 jit_solution(8073803659460172852)
XLA Ops:
  0.6 0.0 copy-start
  0.6 56.7 %skeleton_cg.1 = (f32[16,1024]{1,0:T(8,128)}, f32[16,1024]{1,0:T(8,128)}, f32[16,1024]{1,0:T(8,128)}, f32[16,1024]{1,0:T(8,128)}) custom-call(f32[8,1024]{1,0:T(8,128)} %points_hbm.1, f32[16,1024]{1,0:T(8,128)} %rhs_hbm.1, f32[1024,128]{1,0:T(8,128)} %basis_hbm.1, f32[1,128,128]{2,1,0:T(8,128)} %lift_hbm.1, f32[1,1024]{1,0:T(1,128)} %bitcast.2, ...), custom_call_target="tpu_custom_call" | custom-call | tf_op jit(solution)/shard_map/skeleton_cg/pallas_call | solution.py:540
  57.4 0.0 copy-done
  57.4 1.6 %multiply_add_fusion = (f32[16,1024]{1,0:T(8,128)}, f32[16,1024]{1,0:T(8,128)}) fusion(f32[16,1024]{1,0:T(8,128)} %get-tuple-element.7, f32[16,1024]{1,0:T(8,128)} %get-tuple-element.9, f32[16,1024]{1,0:T(8,128)S(1)} %copy-done, f32[16,1024]{1,0:T(8,128)} %get-tuple-element.6, f32[16,1024]{1,0:T(8,128)} %get-tuple-element.8), kind=kLoop, calls=%fused_computation | loop fusion | flops 114688 | bytes 458752 | tf_op jit(solution)/shard_map/add | solution.py:551
Async XLA Ops:
  0.6 56.8 %copy-start = (f32[16,1024]{1,0:T(8,128)S(1)}, f32[16,1024]{1,0:T(8,128)}, u32[]{:S(2)}) copy-start(f32[16,1024]{1,0:T(8,128)} %rhs_hbm.1) | copy-start | bytes 196612

commit v2 on v1

--- a/solution.py
+++ b/solution.py
@@ -66,14 +66,14 @@
     return (1.0 + scaled * (LN2 + scaled * (LN2 * LN2 / 3.0))) * jnp.exp2(-scaled)
 
 
-def fill_block(left_ref, right_ref, high_ref, low_ref, first=0, last=None):
-    rows, columns = high_ref.shape
-    last = columns if last is None else last
+def fill_block(left_ref, right_ref, high_ref, low_ref, first=0, last=None, top=0, bottom=None):
+    last = high_ref.shape[1] if last is None else last
+    bottom = high_ref.shape[0] if bottom is None else bottom
     wide = min(256, last - first)
-    tall = min(rows, 64 if last - first > 256 else 256)
+    tall = min(bottom - top, 1024 if last - first <= 128 else 512)
 
     def one(index, carry):
-        at = pl.ds(pl.multiple_of(index * tall, tall), tall)
+        at = pl.ds(pl.multiple_of(top + index * tall, tall), tall)
         left = left_ref[at, :]
         for start in range(first, last, wide):
             stop = min(start + wide, last)
@@ -83,7 +83,7 @@
             low_ref[at, start:stop] = low
         return carry
 
-    lax.fori_loop(0, rows // tall, one, 0)
+    lax.fori_loop(0, (bottom - top) // tall, one, 0)
 
 
 def times(first, second, turned=False):
@@ -266,18 +266,13 @@
     def keep(value, high_ref, low_ref):
         high_ref[...], low_ref[...] = two_parts(value)
 
-    loads["rhs"].wait()
-    loads["basis"].wait()
+    for load in loads.values():
+        load.wait()
     rhs = rhs_ref[...]
     keep(basis_ref[...], basis_high, basis_low)
     coeff = product(rhs, basis_high[...], basis_low[...])
-    loads["lift"].wait()
     keep(lift_ref[0], lift_high, lift_low)
     lifted = product(coeff, lift_high[...], lift_low[...])
-    loads["points"].wait()
-    loads["scale"].wait()
-    loads["leaf_skel"].wait()
-    loads["group_skel"].wait()
     diagonal = row_of((8, 8)) == lane_of((8, 8))
     inv_column = jnp.sum(jnp.where(diagonal, scale_ref[...], 0.0), axis=1, keepdims=True) * STRETCH
     own = points_ref[...] * inv_column
@@ -300,8 +295,6 @@
     points_copy = send(points_ref, points_up, along_boxes(-1))
     vec_copy = send(rhs_ref, vec_up.at[0], along_boxes(-1))
 
-    loads["links"].wait()
-    loads["noise"].wait()
     right_bit = links_ref[:, 1:2].astype(F32)
     weight_self = 1.0 + links_ref[:, 0:1].astype(F32) + right_bit
     left_ref[...] = features(own, True).T.astype(BF16)
@@ -324,13 +317,15 @@
     left_ref[: n_y * 128, :] = far_left.astype(BF16)
     far_right = features(side_by_side(cross_1, n_cross, 16, 24), False)
     right_ref[:, : n_cross * 128] = far_right.astype(BF16)
-    fill_block(left_ref, right_ref, far_high, far_low)
+    middle = n_y * 64
+    fill_block(left_ref, right_ref, far_high, far_low, bottom=middle)
 
     arrived(line_2_copies)
     top_3[0, :16, :] = added_up(line_2, n_y, 0, 16)
     top_own = added_up(line_2, n_y, 16, 24)
     top_3[0, 16:, :] = top_own
     top_3_copies = spread(top_3, groups, along_groups)
+    fill_block(left_ref, right_ref, far_high, far_low, top=middle)
 
     def far_terms(spread_out, out, into):
         for slot in range(n_cross):
@@ -446,6 +441,8 @@
         second_ref[...] + product_in[1] + product(row, turned_high[...], turned_low[...])
     )
     top_wu = lane_sum(top_out * top_coeff)
+    for copy in started:
+        copy.wait_send()
     arrived(sums_3_copies)
     total = added_up(sums_3, groups, 0, 8)
     rr, rw, ww, wu = (
@@ -461,9 +458,6 @@
     next_alpha = next_rr / (curve - ratio * next_rr / alpha)
     one_ref[...] = jnp.broadcast_to(alpha + next_alpha * (1.0 + ratio), one_ref.shape)
     two_ref[...] = jnp.broadcast_to(alpha * next_alpha, two_ref.shape)
-
-    for copy in started:
-        copy.wait_send()
 
 
 def copies_of(sizes):

time: 59.2 us -> 52.9 us (0.89)
  Pallas kernels: 56.7 us -> 50.2 us
    pallas_call x1, Pallas kernels: 56.7 us -> 50.2 us  [local(): pl.pallas_call(functools.partial(everything, sizes), name='skeleton_cg',...]
where the time goes in v2:
time: 52.9 us; the launch traced here: 52.4 us
  Pallas kernels  50.2 us (95%)
  other arithmetic  1.61 us (3%)
  between operations  0.66 us (1%)
    pallas_call x1, Pallas kernels, local(): pl.pallas_call(functools.partial(everything, sizes), name='skeleton_cg',...  50.2 us
    add x1, other arithmetic, local(): return (one * rhs - two * image, rhs - one * image + two * second)  1.61 us

profile of v2, /device:TPU:1, one launch (start us, length us, event | category | flops | bytes accessed | tf_op | source)
XLA Modules:
  0.0 52.4 jit_solution(11590156431388993295)
XLA Ops:
  0.6 0.0 copy-start
  0.6 50.2 %skeleton_cg.1 = (f32[16,1024]{1,0:T(8,128)}, f32[16,1024]{1,0:T(8,128)}, f32[16,1024]{1,0:T(8,128)}, f32[16,1024]{1,0:T(8,128)}) custom-call(f32[8,1024]{1,0:T(8,128)} %points_hbm.1, f32[16,1024]{1,0:T(8,128)} %rhs_hbm.1, f32[1024,128]{1,0:T(8,128)} %basis_hbm.1, f32[1,128,128]{2,1,0:T(8,128)} %lift_hbm.1, f32[1,1024]{1,0:T(1,128)} %bitcast.2, ...), custom_call_target="tpu_custom_call" | custom-call | tf_op jit(solution)/shard_map/skeleton_cg/pallas_call | solution.py:534
  50.8 0.0 copy-done
  50.8 1.6 %multiply_add_fusion = (f32[16,1024]{1,0:T(8,128)}, f32[16,1024]{1,0:T(8,128)}) fusion(f32[16,1024]{1,0:T(8,128)} %get-tuple-element.7, f32[16,1024]{1,0:T(8,128)} %get-tuple-element.9, f32[16,1024]{1,0:T(8,128)S(1)} %copy-done, f32[16,1024]{1,0:T(8,128)} %get-tuple-element.6, f32[16,1024]{1,0:T(8,128)} %get-tuple-element.8), kind=kLoop, calls=%fused_computation | loop fusion | flops 114688 | bytes 458752 | tf_op jit(solution)/shard_map/add | solution.py:545
Async XLA Ops:
  0.6 50.2 %copy-start = (f32[16,1024]{1,0:T(8,128)S(1)}, f32[16,1024]{1,0:T(8,128)}, u32[]{:S(2)}) copy-start(f32[16,1024]{1,0:T(8,128)} %rhs_hbm.1) | copy-start | bytes 196612

commit v3 on v2

--- a/solution.py
+++ b/solution.py
@@ -291,8 +291,8 @@
 
     pl.semaphore_wait(barrier, len(partners))
     cross_1_copies = spread(cross_1, n_cross, along_cross)
+    points_copy = send(points_ref, points_up, along_boxes(-1))
     line_1_copies = spread(line_1, n_y, along_line)
-    points_copy = send(points_ref, points_up, along_boxes(-1))
     vec_copy = send(rhs_ref, vec_up.at[0], along_boxes(-1))
 
     right_bit = links_ref[:, 1:2].astype(F32)
@@ -306,7 +306,7 @@
     line_2[0, 16:, :] = added_up(cross_1, n_cross, 24, 32)
     line_2_copies = spread(line_2, n_y, along_line)
 
-    arrived([points_copy, vec_copy])
+    arrived([points_copy])
     right_ref[...] = features(points_up[...] * inv_column, False).astype(BF16)
     fill_block(left_ref, right_ref, link_high, link_low)
     product_out[0] = right_bit * product(rhs, link_high[...], link_low[...])
@@ -352,7 +352,9 @@
     def upper_part(above):
         return right_bit * product(above, link_high[...], link_low[...], True)
 
-    near = self_part(rhs) + upper_part(vec_up[0])
+    near = self_part(rhs)
+    arrived([vec_copy])
+    near = near + upper_part(vec_up[0])
 
     turned = basis_ref[...].T
     keep(turned, turned_high, turned_low)
@@ -401,10 +403,9 @@
     arrived(cross_1b_copies)
     line_2b[0] = added_up(cross_1b, n_cross, 0, 16)
     line_2b_copies = spread(line_2b, n_y, along_line)
+    second_ref[...] = near
     arrived([vec_copy])
-    upper = upper_part(vec_up[1])
-    dot_wu = dot_wu + 2.0 * lane_sum(image * upper)
-    second_ref[...] = near + upper
+    dot_wu = dot_wu + 2.0 * lane_sum(product_out[1] * vec_up[1])
     arrived(line_1b_copies)
     spread_out = product(side_by_side(line_1b, n_y, 0, 16), far_high[...], far_low[...])
     cross_2b_copies = far_terms(spread_out, cross_2b_out, cross_2b_in)
@@ -417,6 +418,7 @@
         packed = jnp.where(lane == index + 4, dot[8:], packed)
     sums_1[0] = packed
     sums_1_copies = spread(sums_1, n_cross, along_cross)
+    second_ref[...] = second_ref[...] + upper_part(vec_up[1])
 
     top_right_ref[...] = features(top_all, False).astype(BF16)
     fill_block(top_left_ref, top_right_ref, top_high, top_low, 128)

time: 52.9 us -> 52.3 us (0.989)
  no operation moved by 1% of the time
where the time goes in v3:
time: 52.3 us; the launch traced here: 52 us
  Pallas kernels  49.7 us (95%)
  other arithmetic  1.61 us (3%)
  between operations  0.66 us (1%)
    pallas_call x1, Pallas kernels, local(): pl.pallas_call(functools.partial(everything, sizes), name='skeleton_cg',...  49.7 us
    add x1, other arithmetic, local(): return (one * rhs - two * image, rhs - one * image + two * second)  1.61 us

profile of v3, /device:TPU:1, one launch (start us, length us, event | category | flops | bytes accessed | tf_op | source)
XLA Modules:
  0.0 52.0 jit_solution(5363053252823439809)
XLA Ops:
  0.6 0.0 copy-start
  0.6 49.7 %skeleton_cg.1 = (f32[16,1024]{1,0:T(8,128)}, f32[16,1024]{1,0:T(8,128)}, f32[16,1024]{1,0:T(8,128)}, f32[16,1024]{1,0:T(8,128)}) custom-call(f32[8,1024]{1,0:T(8,128)} %points_hbm.1, f32[16,1024]{1,0:T(8,128)} %rhs_hbm.1, f32[1024,128]{1,0:T(8,128)} %basis_hbm.1, f32[1,128,128]{2,1,0:T(8,128)} %lift_hbm.1, f32[1,1024]{1,0:T(1,128)} %bitcast.2, ...), custom_call_target="tpu_custom_call" | custom-call | tf_op jit(solution)/shard_map/skeleton_cg/pallas_call | solution.py:536
  50.4 0.0 copy-done
  50.4 1.6 %multiply_add_fusion = (f32[16,1024]{1,0:T(8,128)}, f32[16,1024]{1,0:T(8,128)}) fusion(f32[16,1024]{1,0:T(8,128)} %get-tuple-element.7, f32[16,1024]{1,0:T(8,128)} %get-tuple-element.9, f32[16,1024]{1,0:T(8,128)S(1)} %copy-done, f32[16,1024]{1,0:T(8,128)} %get-tuple-element.6, f32[16,1024]{1,0:T(8,128)} %get-tuple-element.8), kind=kLoop, calls=%fused_computation | loop fusion | flops 114688 | bytes 458752 | tf_op jit(solution)/shard_map/add | solution.py:547
Async XLA Ops:
  0.6 49.7 %copy-start = (f32[16,1024]{1,0:T(8,128)S(1)}, f32[16,1024]{1,0:T(8,128)}, u32[]{:S(2)}) copy-start(f32[16,1024]{1,0:T(8,128)} %rhs_hbm.1) | copy-start | bytes 196612

commit v4 on v3

--- a/solution.py
+++ b/solution.py
@@ -128,6 +128,10 @@
     links_hbm,
     leaf_skel_hbm,
     group_skel_hbm,
+    image_hbm,
+    second_hbm,
+    one_hbm,
+    two_hbm,
     image_ref,
     second_ref,
     one_ref,
@@ -394,6 +398,8 @@
     image = image_ref[...] + product(row, turned_high[...], turned_low[...])
     image_ref[...] = image
     vec_copy = send(image_ref, vec_up.at[1], along_boxes(-1))
+    image_out = pltpu.make_async_copy(image_ref, image_hbm, load_sem.at[9])
+    image_out.start()
     product_out[1] = right_bit * product(image, link_high[...], link_low[...])
     product_copy = send(product_out.at[1], product_in.at[1], along_boxes(1))
     near = self_part(image)
@@ -442,9 +448,13 @@
     second_ref[...] = (
         second_ref[...] + product_in[1] + product(row, turned_high[...], turned_low[...])
     )
+    second_out = pltpu.make_async_copy(second_ref, second_hbm, load_sem.at[10])
+    second_out.start()
     top_wu = lane_sum(top_out * top_coeff)
     for copy in started:
         copy.wait_send()
+    image_out.wait()
+    second_out.wait()
     arrived(sums_3_copies)
     total = added_up(sums_3, groups, 0, 8)
     rr, rw, ww, wu = (
@@ -459,7 +469,13 @@
     ratio = next_rr / rr
     next_alpha = next_rr / (curve - ratio * next_rr / alpha)
     one_ref[...] = jnp.broadcast_to(alpha + next_alpha * (1.0 + ratio), one_ref.shape)
+    one_out = pltpu.make_async_copy(one_ref, one_hbm, load_sem.at[11])
+    one_out.start()
     two_ref[...] = jnp.broadcast_to(alpha * next_alpha, two_ref.shape)
+    two_out = pltpu.make_async_copy(two_ref, two_hbm, load_sem.at[12])
+    two_out.start()
+    one_out.wait()
+    two_out.wait()
 
 
 def copies_of(sizes):
@@ -494,6 +510,7 @@
         return [pltpu.VMEM(shape, BF16)] * 2
 
     scratch = [
+        *[held(rows, width)] * 4,
         *[pltpu.VMEM(operand.shape, operand.dtype) for operand in operands],
         pltpu.VMEM((width, FEATURES), BF16),
         pltpu.VMEM((FEATURES, width), BF16),
@@ -528,17 +545,16 @@
         held(n_cross, 8, skel),
         held(n_y, 8, skel),
         held(groups, 8, skel),
-        pltpu.SemaphoreType.DMA((len(operands),)),
+        pltpu.SemaphoreType.DMA((len(operands) + 4,)),
         pltpu.SemaphoreType.DMA((count,)),
         pltpu.SemaphoreType.DMA((count,)),
     ]
-    vmem = pl.BlockSpec(memory_space=pltpu.VMEM)
     image, second, one, two = pl.pallas_call(
         functools.partial(everything, sizes),
         name="skeleton_cg",
         out_shape=[jax.ShapeDtypeStruct(rhs.shape, F32)] * 4,
         in_specs=[pl.BlockSpec(memory_space=pltpu.HBM)] * len(operands),
-        out_specs=[vmem] * 4,
+        out_specs=[pl.BlockSpec(memory_space=pltpu.HBM)] * 4,
         scratch_shapes=scratch,
         compiler_params=pltpu.CompilerParams(
             collective_id=0, has_side_effects=True

time: 52.3 us -> 52.3 us (level)
  no operation moved by 1% of the time
where the time goes in v4:
time: 52.3 us; the launch traced here: 52 us
  Pallas kernels  49.8 us (95%)
  other arithmetic  1.61 us (3%)
  between operations  0.66 us (1%)
    pallas_call x1, Pallas kernels, local(): pl.pallas_call(functools.partial(everything, sizes), name='skeleton_cg',...  49.8 us
    add x1, other arithmetic, local(): return (one * rhs - two * image, rhs - one * image + two * second)  1.61 us

profile of v4, /device:TPU:1, one launch (start us, length us, event | category | flops | bytes accessed | tf_op | source)
XLA Modules:
  0.0 52.0 jit_solution(15666893555403299655)
XLA Ops:
  0.6 0.0 copy-start
  0.6 49.8 %skeleton_cg.1 = (f32[16,1024]{1,0:T(8,128)}, f32[16,1024]{1,0:T(8,128)}, f32[16,1024]{1,0:T(8,128)}, f32[16,1024]{1,0:T(8,128)}) custom-call(f32[8,1024]{1,0:T(8,128)} %points_hbm.1, f32[16,1024]{1,0:T(8,128)} %rhs_hbm.1, f32[1024,128]{1,0:T(8,128)} %basis_hbm.1, f32[1,128,128]{2,1,0:T(8,128)} %lift_hbm.1, f32[1,1024]{1,0:T(1,128)} %bitcast.2, ...), custom_call_target="tpu_custom_call" | custom-call | tf_op jit(solution)/shard_map/skeleton_cg/pallas_call | solution.py:552
  50.4 0.0 copy-done
  50.4 1.6 %multiply_add_fusion = (f32[16,1024]{1,0:T(8,128)}, f32[16,1024]{1,0:T(8,128)}) fusion(f32[16,1024]{1,0:T(8,128)} %get-tuple-element.7, f32[16,1024]{1,0:T(8,128)} %get-tuple-element.9, f32[16,1024]{1,0:T(8,128)S(1)} %copy-done, f32[16,1024]{1,0:T(8,128)} %get-tuple-element.6, f32[16,1024]{1,0:T(8,128)} %get-tuple-element.8), kind=kLoop, calls=%fused_computation | loop fusion | flops 114688 | bytes 458752 | tf_op jit(solution)/shard_map/add | solution.py:563
Async XLA Ops:
  0.6 49.8 %copy-start = (f32[16,1024]{1,0:T(8,128)S(1)}, f32[16,1024]{1,0:T(8,128)}, u32[]{:S(2)}) copy-start(f32[16,1024]{1,0:T(8,128)} %rhs_hbm.1) | copy-start | bytes 196612
